TPU v7x, 32 devices: a whole 2x2x4 slice. The times are simulated.
32 devices in a mesh: grp: 2 (over y), seq: 4 (over z), head: 4 (over x, core).
Axes of the slice: x: 2, y: 2, z: 4, core: 2. Of those that a mesh axis runs over, the one named last changes fastest.
Arguments:
- queries: bfloat16 [1024, 32, 128], P(('grp', 'seq'), 'head'), parts along dimension 0, may hold values from -26 to 26
- keys: bfloat16 [1024, 8, 128], P(('grp', 'seq'), 'head'), parts along dimension 0, may hold values from -13 to 13
- values: bfloat16 [1024, 8, 128], P(('grp', 'seq'), 'head'), parts along dimension 0, may hold values from -6 to 6
- block_order: int32 [16], P('grp'), parts along dimension 0, may hold values from 0 to 7, as said below
Outputs:
- attended: bfloat16 [1024, 32, 128], P(('grp', 'seq'), 'head'), parts along dimension 0
There are 2 independent parts, one for each index of `grp`. A program takes and returns all parts, laid end to end along the dimension named above; each array names one. Nothing has to cross between parts.
Inputs may be any that keep to these rules, and one draw needn't show every extreme that they name: `block_order`: slots 2 i and 2 i + 1 hold blocks c and 7 - c for some c, in either order; every block stands in one slot.
All inputs are finite; a program needn't handle non-finite values.
Results may differ from a plain program's by a relative error of at most 0.0055.
Values may be sent and summed in bfloat16 or wider, within the bound.
A program may use at most 128 MiB of HBM per device.

v0:
```python
import jax
import jax.numpy as jnp
from jax import lax
from jax.sharding import PartitionSpec as P


def partner(value, axis, stride):
    mask = 2**stride
    pairs = [(source, source ^ mask) for source in range(lax.axis_size(axis))]
    return lax.ppermute(value, axis, pairs)


def from_behind(value, axis, by):
    devices = lax.axis_size(axis)
    return lax.ppermute(value, axis, [(i, (i + by) % devices) for i in range(devices)])


def locate(table, start, count, half_rows):
    index = start + jnp.arange(count, dtype=jnp.int32)
    slot = index // half_rows
    match = slot[:, None] == jnp.arange(table.shape[0], dtype=jnp.int32)[None, :]
    block_id = jnp.sum(jnp.where(match, table[None, :], 0), axis=1)
    return block_id * half_rows + index % half_rows


def attend(state, query_rows, query_pos, key_rows, value_rows, key_pos, score_scale):
    running_max, running_sum, running_acc = state
    scores = (
        jnp.einsum("cghd,pgd->ghcp", query_rows, key_rows, preferred_element_type=jnp.float32)
        * score_scale
    )
    visible = (key_pos[None, :] <= query_pos[:, None])[None, None]
    new_max = jnp.maximum(running_max, jnp.max(jnp.where(visible, scores, -1e30), axis=-1))
    weights = jnp.where(visible, jnp.exp(scores - new_max[..., None]), 0.0)
    factor = jnp.exp(running_max - new_max)
    new_sum = running_sum * factor + jnp.sum(weights, axis=-1)
    product = jnp.einsum(
        "ghcp,pgd->ghcd",
        weights.astype(jnp.bfloat16),
        value_rows,
        preferred_element_type=jnp.float32,
    )
    new_acc = running_acc * factor[..., None] + product
    return (new_max, new_sum, new_acc)


def finish(state, half_rows):
    running_max, running_sum, running_acc = state
    result = running_acc / running_sum[..., None]
    groups = result.shape[0] * result.shape[1]
    return (
        jnp.transpose(result, (2, 0, 1, 3))
        .reshape(half_rows, groups, result.shape[3])
        .astype(jnp.bfloat16)
    )


def fresh_state(groups, per_group, half_rows, head_width):
    return (
        jnp.full((groups, per_group, half_rows), -1e30, jnp.float32),
        jnp.zeros((groups, per_group, half_rows), jnp.float32),
        jnp.zeros((groups, per_group, half_rows, head_width), jnp.float32),
    )


def on_device(queries, keys, values, block_order):
    tokens = queries.shape[0]
    half_rows = tokens // 2
    groups = keys.shape[1]
    per_group = queries.shape[1] // groups
    head_width = queries.shape[2]
    score_scale = head_width ** (-0.5)
    seq_index = lax.axis_index("seq")
    half_groups = groups // 2
    half_heads = half_groups * per_group
    parity = seq_index % 2
    pair_index = seq_index // 2
    pair_total = lax.axis_size("seq") // 2
    own_q = lax.dynamic_slice_in_dim(queries, parity * half_heads, half_heads, 1)
    own_k = lax.dynamic_slice_in_dim(keys, parity * half_groups, half_groups, 1)
    own_v = lax.dynamic_slice_in_dim(values, parity * half_groups, half_groups, 1)
    other_q = lax.dynamic_slice_in_dim(queries, (1 - parity) * half_heads, half_heads, 1)
    other_k = lax.dynamic_slice_in_dim(keys, (1 - parity) * half_groups, half_groups, 1)
    other_v = lax.dynamic_slice_in_dim(values, (1 - parity) * half_groups, half_groups, 1)
    got_q, got_k, got_v = partner((other_q, other_k, other_v), "seq", 0)
    lower = parity == 0
    pair_q = jnp.where(
        lower, jnp.concatenate([own_q, got_q], 0), jnp.concatenate([got_q, own_q], 0)
    )
    pair_k = jnp.where(
        lower, jnp.concatenate([own_k, got_k], 0), jnp.concatenate([got_k, own_k], 0)
    )
    pair_v = jnp.where(
        lower, jnp.concatenate([own_v, got_v], 0), jnp.concatenate([got_v, own_v], 0)
    )
    pair_rows = 2 * tokens
    split_q = pair_q.reshape(4, half_rows, half_groups, per_group, head_width)
    pair_pos = locate(block_order, pair_index * pair_rows, pair_rows, half_rows)
    query_blocks = [pair_pos[which * half_rows : (which + 1) * half_rows] for which in range(4)]

    def consume(states, key_rows, value_rows, source):
        key_pos = locate(block_order, source * pair_rows, pair_rows, half_rows)
        result = []
        for which in range(4):
            state = states[which]
            for piece in range(4):
                low = piece * half_rows
                state = attend(
                    state,
                    split_q[which],
                    query_blocks[which],
                    key_rows[low : low + half_rows],
                    value_rows[low : low + half_rows],
                    key_pos[low : low + half_rows],
                    score_scale,
                )
            result.append(state)
        return tuple(result)

    states = tuple(
        (fresh_state(half_groups, per_group, half_rows, head_width) for which in range(4))
    )
    states = consume(states, pair_k, pair_v, pair_index)

    def pass_step(step, carry):
        states, key_rows, value_rows = carry
        key_rows, value_rows = from_behind((key_rows, value_rows), "seq", 2)
        source = (pair_index - step) % pair_total
        return (consume(states, key_rows, value_rows, source), key_rows, value_rows)

    states, ignored_k, ignored_v = lax.fori_loop(1, pair_total, pass_step, (states, pair_k, pair_v))
    outputs = jnp.concatenate([finish(states[which], half_rows) for which in range(4)], axis=0)
    first_rows = outputs[:tokens]
    second_rows = outputs[tokens:]
    mine = jnp.where(lower, first_rows, second_rows)
    theirs = jnp.where(lower, second_rows, first_rows)
    returned = partner(theirs, "seq", 0)
    return jnp.where(
        lower, jnp.concatenate([mine, returned], 1), jnp.concatenate([returned, mine], 1)
    )


def solution(mesh):
    placed = (
        P(("grp", "seq"), "head", None),
        P(("grp", "seq"), "head", None),
        P(("grp", "seq"), "head", None),
        P("grp"),
    )
    return jax.shard_map(
        on_device,
        mesh=mesh,
        in_specs=placed,
        out_specs=P(("grp", "seq"), "head", None),
        check_vma=False,
    )
```

profile of v0, /device:TPU:0, one launch (start us, length us, event | category | flops | bytes accessed | tf_op | source)
XLA Modules:
  0.0 33.9 jit_solution(1314867537099419183)
XLA Ops:
  0.0 1.2 %constant_dynamic-slice_fusion.3 = (bf16[128,4,128]{2,1,0:T(4,128)(2,1)S(1)}, bf16[128,4,128]{2,1,0:T(4,128)(2,1)S(1)}) fusion(bf16[128,8,128]{2,1,0:T(8,128)(2,1)} %param.4, s32[]{:T(128)S(6)} %select_n.365, s32[]{:T(128)S(6)} %select_n.366), kind=kLoop, calls=%fused_computation.545 | loop fusion | bytes 524296 | tf_op jit(solution)/shard_map/dynamic_slice | solution.py:79
  1.2 3.1 %collective-permute-start.1 = (bf16[128,4,128]{2,0,1:T(8,128)(2,1)S(1)}, bf16[128,4,128]{2,0,1:T(8,128)(2,1)S(1)}, u32[]{:S(2)}, u32[]{:S(2)}) collective-permute-start(bf16[128,4,128]{2,0,1:T(8,128)(2,1)S(1)} %copy.118), channel_id=1, source_target_pairs={{0,4},{4,0},{8,12},{12,8},{1,5},{5,1},{9,13},{13,9},{2,6},{6,2},{1... | collective-permute-start | bytes 393224 | tf_op jit(solution)/shard_map/ppermute | solution.py:10
  4.5 0.8 %collective-permute-start = (bf16[128,1,128]{2,0,1:T(8,128)(2,1)S(1)}, bf16[128,1,128]{2,0,1:T(8,128)(2,1)S(1)}, u32[]{:S(2)}, u32[]{:S(2)}) collective-permute-start(bf16[128,1,128]{2,0,1:T(8,128)(2,1)S(1)} %copy.116), channel_id=1, source_target_pairs={{0,4},{4,0},{8,12},{12,8},{1,5},{5,1},{9,13},{13,9},{2,6},{6,2},{1... | collective-permute-start | bytes 98312 | tf_op jit(solution)/shard_map/ppermute | solution.py:10
  5.5 1.3 %collective-permute-start.2 = (bf16[128,1,128]{2,0,1:T(8,128)(2,1)S(1)}, bf16[128,1,128]{2,0,1:T(8,128)(2,1)S(1)}, u32[]{:S(2)}, u32[]{:S(2)}) collective-permute-start(bf16[128,1,128]{2,0,1:T(8,128)(2,1)S(1)} %copy.120), channel_id=1, source_target_pairs={{0,4},{4,0},{8,12},{12,8},{1,5},{5,1},{9,13},{13,9},{2,6},{6,2},{1... | collective-permute-start | bytes 98312 | tf_op jit(solution)/shard_map/ppermute | solution.py:10
  6.8 0.6 %copy-done.2 = s32[8]{0:T(128)S(1)} copy-done((s32[8]{0:T(128)S(1)}, s32[8]{0:T(128)}, u32[]{:S(2)}) %copy-start.2) | copy-done | bytes 56
  7.8 0.2 broadcast_compare_fusion.30
  8.0 0.8 %collective-permute-done = bf16[128,1,128]{2,0,1:T(8,128)(2,1)S(1)} collective-permute-done((bf16[128,1,128]{2,0,1:T(8,128)(2,1)S(1)}, bf16[128,1,128]{2,0,1:T(8,128)(2,1)S(1)}, u32[]{:S(2)}, u32[]{:S(2)}) %collective-permute-start) | collective-permute-done | bytes 32800 | tf_op jit(solution)/shard_map/ppermute | solution.py:10
  8.9 2.8 %collective-permute-start.3 = (bf16[256,1,128]{2,0,1:T(8,128)(2,1)S(1)}, bf16[256,1,128]{2,0,1:T(8,128)(2,1)S(1)}, u32[]{:S(2)}, u32[]{:S(2)}) collective-permute-start(bf16[256,1,128]{2,0,1:T(8,128)(2,1)S(1)} %maximum_select_fusion.2), channel_id=1, source_target_pairs={{0,8},{4,12},{8,0},{12,4},{1,9},{5,13},{9,1},{13,5},{2,10},{6,14},... | collective-permute-start | bytes 196616 | tf_op jit(solution)/shard_map/while/body/eval_jaxpr/ppermute | solution.py:15
  11.7 0.4 %collective-permute-start.4 = (bf16[256,1,128]{2,0,1:T(8,128)(2,1)S(1)}, bf16[256,1,128]{2,0,1:T(8,128)(2,1)S(1)}, u32[]{:S(2)}, u32[]{:S(2)}) collective-permute-start(bf16[256,1,128]{2,0,1:T(8,128)(2,1)S(1)} %maximum_select_fusion.3), channel_id=1, source_target_pairs={{0,8},{4,12},{8,0},{12,4},{1,9},{5,13},{9,1},{13,5},{2,10},{6,14},... | collective-permute-start | bytes 196616 | tf_op jit(solution)/shard_map/while/body/eval_jaxpr/ppermute | solution.py:15
  12.4 0.2 select_reduce_fusion.29
  13.1 0.2 select_reduce_fusion.20
  16.9 0.2 fusion.74
  17.1 0.2 fusion.72
  17.3 0.2 fusion.70
  17.6 0.2 fusion.68
  17.8 0.2 select_reduce_fusion.16
  19.1 0.2 fusion.55
  19.3 0.2 fusion.53
  19.5 0.2 fusion.51
  19.7 0.2 fusion.49
  19.9 0.2 select_reduce_fusion.8
  21.2 0.2 fusion.36
  21.5 0.2 fusion.34
  21.7 0.2 fusion.32
  21.9 0.2 fusion.30
  22.1 0.2 select_reduce_fusion.3
  23.4 0.2 fusion.17
  23.6 0.2 fusion.15
  23.8 0.2 fusion.13
  24.0 0.2 fusion.11
  24.5 0.2 fusion.209
  24.7 0.2 fusion.206
  24.9 0.2 fusion.193
  25.1 0.2 fusion.190
  25.3 0.2 fusion.187
  25.5 0.2 fusion.174
  25.7 0.2 fusion.171
  25.9 0.2 fusion.168
  26.2 0.2 fusion.155
  26.4 0.2 fusion.152
  26.6 0.2 fusion.149
  26.8 0.3 fusion.83
  27.1 0.3 fusion.82
  27.3 0.3 fusion.81
  27.6 0.3 fusion.80
  28.0 1.7 %collective-permute-start.5 = (bf16[128,4,128]{2,0,1:T(8,128)(2,1)S(1)}, bf16[128,4,128]{2,0,1:T(8,128)(2,1)S(1)}, u32[]{:S(2)}, u32[]{:S(2)}) collective-permute-start(bf16[128,4,128]{2,0,1:T(8,128)(2,1)S(1)} %get-tuple-element.137), channel_id=1, source_target_pairs={{0,4},{4,0},{8,12},{12,8},{1,5},{5,1},{9,13},{13,9},{2,6},{6,2},{1... | collective-permute-start | bytes 393224 | tf_op jit(solution)/shard_map/ppermute | solution.py:10
  29.6 3.4 %collective-permute-done.5 = bf16[128,4,128]{2,0,1:T(8,128)(2,1)S(1)} collective-permute-done((bf16[128,4,128]{2,0,1:T(8,128)(2,1)S(1)}, bf16[128,4,128]{2,0,1:T(8,128)(2,1)S(1)}, u32[]{:S(2)}, u32[]{:S(2)}) %collective-permute-start.5) | collective-permute-done | bytes 131104 | tf_op jit(solution)/shard_map/ppermute | solution.py:10
  33.0 0.9 %copy.82 = bf16[128,8,128]{2,1,0:T(8,128)(2,1)} copy(bf16[128,8,128]{2,0,1:T(8,128)(2,1)S(1)} %maximum_select_fusion.1) | data formatting | bytes 524288 | tf_op jit(solution)/shard_map/jit(_where)/select_n | solution.py:138
  (96 shorter events, 8.4 us)
Async XLA Ops:
  1.2 3.2 %copy-start = (bf16[128,2,128]{2,1,0:T(2,128)(2,1)S(1)}, bf16[128,2,128]{2,1,0:T(2,128)(2,1)}, u32[]{:S(2)}) copy-start(bf16[128,2,128]{2,1,0:T(2,128)(2,1)} %param.5) | copy-start | bytes 196612
  1.2 10.9 %collective-permute-start.1 = (bf16[128,4,128]{2,0,1:T(8,128)(2,1)S(1)}, bf16[128,4,128]{2,0,1:T(8,128)(2,1)S(1)}, u32[]{:S(2)}, u32[]{:S(2)}) collective-permute-start(bf16[128,4,128]{2,0,1:T(8,128)(2,1)S(1)} %copy.118), channel_id=1, source_target_pairs={{0,4},{4,0},{8,12},{12,8},{1,5},{5,1},{9,13},{13,9},{2,6},{6,2},{1... | collective-permute-start | bytes 393224 | tf_op jit(solution)/shard_map/ppermute | solution.py:10
  4.5 0.8 %copy-start.1 = (bf16[128,2,128]{2,1,0:T(2,128)(2,1)S(1)}, bf16[128,2,128]{2,1,0:T(2,128)(2,1)}, u32[]{:S(2)}) copy-start(bf16[128,2,128]{2,1,0:T(2,128)(2,1)} %param.6) | copy-start | bytes 196612
  4.5 4.4 %collective-permute-start = (bf16[128,1,128]{2,0,1:T(8,128)(2,1)S(1)}, bf16[128,1,128]{2,0,1:T(8,128)(2,1)S(1)}, u32[]{:S(2)}, u32[]{:S(2)}) collective-permute-start(bf16[128,1,128]{2,0,1:T(8,128)(2,1)S(1)} %copy.116), channel_id=1, source_target_pairs={{0,4},{4,0},{8,12},{12,8},{1,5},{5,1},{9,13},{13,9},{2,6},{6,2},{1... | collective-permute-start | bytes 98312 | tf_op jit(solution)/shard_map/ppermute | solution.py:10
  5.5 6.2 %collective-permute-start.2 = (bf16[128,1,128]{2,0,1:T(8,128)(2,1)S(1)}, bf16[128,1,128]{2,0,1:T(8,128)(2,1)S(1)}, u32[]{:S(2)}, u32[]{:S(2)}) collective-permute-start(bf16[128,1,128]{2,0,1:T(8,128)(2,1)S(1)} %copy.120), channel_id=1, source_target_pairs={{0,4},{4,0},{8,12},{12,8},{1,5},{5,1},{9,13},{13,9},{2,6},{6,2},{1... | collective-permute-start | bytes 98312 | tf_op jit(solution)/shard_map/ppermute | solution.py:10
  6.8 0.7 %copy-start.2 = (s32[8]{0:T(128)S(1)}, s32[8]{0:T(128)}, u32[]{:S(2)}) copy-start(s32[8]{0:T(128)} %param.7) | copy-start | bytes 100
  8.9 6.7 %collective-permute-start.3 = (bf16[256,1,128]{2,0,1:T(8,128)(2,1)S(1)}, bf16[256,1,128]{2,0,1:T(8,128)(2,1)S(1)}, u32[]{:S(2)}, u32[]{:S(2)}) collective-permute-start(bf16[256,1,128]{2,0,1:T(8,128)(2,1)S(1)} %maximum_select_fusion.2), channel_id=1, source_target_pairs={{0,8},{4,12},{8,0},{12,4},{1,9},{5,13},{9,1},{13,5},{2,10},{6,14},... | collective-permute-start | bytes 196616 | tf_op jit(solution)/shard_map/while/body/eval_jaxpr/ppermute | solution.py:15
  11.7 12.5 %collective-permute-start.4 = (bf16[256,1,128]{2,0,1:T(8,128)(2,1)S(1)}, bf16[256,1,128]{2,0,1:T(8,128)(2,1)S(1)}, u32[]{:S(2)}, u32[]{:S(2)}) collective-permute-start(bf16[256,1,128]{2,0,1:T(8,128)(2,1)S(1)} %maximum_select_fusion.3), channel_id=1, source_target_pairs={{0,8},{4,12},{8,0},{12,4},{1,9},{5,13},{9,1},{13,5},{2,10},{6,14},... | collective-permute-start | bytes 196616 | tf_op jit(solution)/shard_map/while/body/eval_jaxpr/ppermute | solution.py:15
  28.0 5.0 %collective-permute-start.5 = (bf16[128,4,128]{2,0,1:T(8,128)(2,1)S(1)}, bf16[128,4,128]{2,0,1:T(8,128)(2,1)S(1)}, u32[]{:S(2)}, u32[]{:S(2)}) collective-permute-start(bf16[128,4,128]{2,0,1:T(8,128)(2,1)S(1)} %get-tuple-element.137), channel_id=1, source_target_pairs={{0,4},{4,0},{8,12},{12,8},{1,5},{5,1},{9,13},{13,9},{2,6},{6,2},{1... | collective-permute-start | bytes 393224 | tf_op jit(solution)/shard_map/ppermute | solution.py:10
where the time goes:
time: 34.1 us; the launch traced here: 33.9 us
  matrix products  13.6 us (40%)
  starting transfers between devices  10.1 us (30%)
  waiting for transfers between devices  4.23 us (12%)
  local copies, waits for them, and re-layouts  3.22 us (9%)
  other arithmetic  2.32 us (7%)
  between operations  0.38 us (1%)
    dot_general x32, matrix products, attend(): jnp.einsum('ghcp,pgd->ghcd', weights.astype(jnp.bfloat16), value_rows, pr...  6.99 us
    ppermute x4, starting transfers between devices, partner(): return lax.ppermute(value, axis, pairs)  6.91 us
    dot_general x32, matrix products, attend(): jnp.einsum('cghd,pgd->ghcp', query_rows, key_rows, preferred_element_type...  6.64 us
    ppermute x4, waiting for transfers between devices, partner(): return lax.ppermute(value, axis, pairs)  4.22 us
    ppermute x2, starting transfers between devices, from_behind(): lax.ppermute(value, axis, [(i, (i + by) % devices) for i in range(devices)])  3.21 us
    reduce_sum x32, other arithmetic, attend(): new_sum = running_sum * factor + jnp.sum(weights, axis=-1)  1.57 us
    dynamic_slice x1, local copies, waits for them, and re-layouts, on_device(): lax.dynamic_slice_in_dim(queries, parity * half_heads, half_heads, 1)  1.17 us
    select_n x1, local copies, waits for them, and re-layouts, on_device(): jnp.where(lower, jnp.concatenate([mine, returned], 1), jnp.concatenate([r...  0.88 us
  transfers between devices with their start and end apart: 6, of which 2 were waited for; matrix products, arithmetic and copies ran while one was open for 38% of the time, Pallas kernels for 0%

commit v1 on v0

v1 whole, which is shorter than its diff:
```python
import functools
import math

import jax
import jax.numpy as jnp
from jax import lax
from jax.experimental import pallas as pl
from jax.experimental.pallas import tpu as pltpu
from jax.sharding import PartitionSpec as P

MESH = pl.DeviceIdType.MESH
NEG = -1e30


def gather_attend(
    n,
    heads,
    groups,
    tile,
    table_ref,
    q_hbm,
    k_hbm,
    v_hbm,
    out_ref,
    q_ref,
    kv_ref,
    p_ref,
    m_ref,
    l_ref,
    acc_ref,
    load_sem,
    send_sem,
    recv_sem,
):
    me = lax.axis_index("seq")
    rows, width = q_ref.shape
    tokens = rows // heads
    half = tokens // 2
    per_group = heads // groups
    cols = tokens * groups
    piece = cols // 2
    factor_scale = width ** (-0.5) * math.log2(math.e)
    right, left = me + 1, me - 1
    has_right, has_left = me < n - 1, me > 0
    interior = jnp.logical_and(has_right, has_left)

    loads = [
        pltpu.make_async_copy(k_hbm, kv_ref.at[me, 0], load_sem.at[0]),
        pltpu.make_async_copy(v_hbm, kv_ref.at[me, 1], load_sem.at[1]),
        pltpu.make_async_copy(q_hbm, q_ref, load_sem.at[2]),
    ]
    for load in loads:
        load.start()

    barrier = pltpu.get_barrier_semaphore()

    @pl.when(has_right)
    def _():
        pl.semaphore_signal(barrier, inc=1, device_id={"seq": right}, device_id_type=MESH)

    @pl.when(has_left)
    def _():
        pl.semaphore_signal(barrier, inc=1, device_id={"seq": left}, device_id_type=MESH)

    pl.semaphore_wait(barrier, has_right.astype(jnp.int32) + has_left.astype(jnp.int32))

    def part(shard, which):
        return kv_ref.at[shard, which // 2, pl.ds((which % 2) * piece, piece)]

    def remote(shard, which, way, target):
        return pltpu.make_async_remote_copy(
            src_ref=part(shard, which),
            dst_ref=part(shard, which),
            send_sem=send_sem.at[way, shard, which],
            recv_sem=recv_sem.at[shard, which],
            device_id={"seq": target},
            device_id_type=MESH,
        )

    for kind in range(2):
        loads[kind].wait()
        for which in (2 * kind, 2 * kind + 1):

            @pl.when(has_right)
            def _():
                remote(me, which, 0, right).start()

            @pl.when(has_left)
            def _():
                remote(me, which, 1, left).start()

    m_ref[...] = jnp.full(m_ref.shape, NEG, jnp.float32)
    l_ref[...] = jnp.zeros(l_ref.shape, jnp.float32)
    acc_ref[...] = jnp.zeros(acc_ref.shape, jnp.float32)
    loads[2].wait()

    paired = jnp.minimum(me, n - 1 - me)

    def arrival(step):
        near = (step + 1) // 2
        both = jnp.where(step % 2 == 1, me - near, me + near)
        one = jnp.where(me < n - 1 - me, me + step - paired, me - step + paired)
        return jnp.where(step <= 2 * paired, both, one)

    def route(shard):
        from_left = shard < me
        way = jnp.where(from_left, 0, 1)
        return way, jnp.where(from_left, right, left)

    lane = lax.broadcasted_iota(jnp.int32, (heads, cols), 1)
    head = lax.broadcasted_iota(jnp.int32, (heads, cols), 0)
    matched = lane % groups == head // per_group
    key_token = lane // groups

    def receive(shard, which):
        remote(shard, which, 0, me).wait_recv()

    def pass_on(shard, which):
        way, target = route(shard)

        @pl.when(interior)
        def _():
            remote(shard, which, way, target).start()

    def scores(shard):
        first, second = table_ref[2 * shard], table_ref[2 * shard + 1]
        key_pos = jnp.where(
            key_token < half, first * half + key_token, (second - 1) * half + key_token
        )
        key_code = jnp.where(matched, key_pos, 2**30)
        key_rows = kv_ref[shard, 0]
        for start in range(0, tokens, tile):
            span = pl.ds(start * heads, tile * heads)
            block = table_ref[2 * me + start // half]
            offset = block * half + start % half
            raw = lax.dot_general(
                q_ref[span, :],
                key_rows,
                (((1,), (1,)), ((), ())),
                preferred_element_type=jnp.float32,
            )
            shaped = raw.reshape(tile, heads, cols)
            query_pos = lax.broadcasted_iota(jnp.int32, shaped.shape, 0) + offset
            shaped = jnp.where(key_code[None] <= query_pos, shaped, NEG)
            raw = shaped.reshape(tile * heads, cols)
            old_max = m_ref[span, :]
            new_max = jnp.maximum(old_max, jnp.max(raw, axis=-1, keepdims=True))
            fade = jnp.exp2((old_max - new_max) * factor_scale)
            total = l_ref[span, :] * fade
            for low in range(0, cols, width):
                weights = jnp.exp2((raw[:, low : low + width] - new_max) * factor_scale)
                total += weights
                p_ref[span, low : low + width] = weights.astype(p_ref.dtype)
            m_ref[span, :] = new_max
            l_ref[span, :] = total
            acc_ref[span, :] = acc_ref[span, :] * fade

    def weigh(shard):
        value_rows = kv_ref[shard, 1]
        for start in range(0, tokens, tile):
            span = pl.ds(start * heads, tile * heads)
            acc_ref[span, :] += jnp.dot(
                p_ref[span, :], value_rows, preferred_element_type=jnp.float32
            )

    def step(index, carry):
        shard = arrival(index)
        received = index > 0

        @pl.when(received)
        def _():
            for which in (0, 1):
                receive(shard, which)
                pass_on(shard, which)

        @pl.when(jnp.logical_and(received, interior))
        def _():
            for which in (2, 3):
                receive(shard, which)
                pass_on(shard, which)

        scores(shard)

        @pl.when(jnp.logical_and(received, jnp.logical_not(interior)))
        def _():
            for which in (2, 3):
                receive(shard, which)

        weigh(shard)
        return carry

    lax.fori_loop(0, n, step, 0)

    for start in range(0, tokens, tile):
        span = pl.ds(start * heads, tile * heads)
        total = jnp.sum(l_ref[span, :], axis=-1, keepdims=True)
        out_ref[span, :] = (acc_ref[span, :] / total).astype(out_ref.dtype)

    def settle(index, carry):
        shard = arrival(index)

        @pl.when(interior)
        def _():
            way, target = route(shard)
            for which in range(4):
                remote(shard, which, way, target).wait_send()

        return carry

    for which in range(4):

        @pl.when(has_right)
        def _():
            remote(me, which, 0, right).wait_send()

        @pl.when(has_left)
        def _():
            remote(me, which, 1, left).wait_send()

    lax.fori_loop(1, n, settle, 0)


def on_device(queries, keys, values, block_order):
    n = lax.axis_size("seq")
    tokens, heads, width = queries.shape
    groups = keys.shape[1]
    rows, cols = tokens * heads, tokens * groups
    tile = min(32, tokens // 2)
    anywhere = pl.BlockSpec(memory_space=pl.ANY)
    out = pl.pallas_call(
        functools.partial(gather_attend, n, heads, groups, tile),
        out_shape=jax.ShapeDtypeStruct((rows, width), queries.dtype),
        in_specs=[pl.BlockSpec(memory_space=pltpu.SMEM), anywhere, anywhere, anywhere],
        out_specs=pl.BlockSpec(memory_space=pltpu.VMEM),
        scratch_shapes=[
            pltpu.VMEM((rows, width), queries.dtype),
            pltpu.VMEM((n, 2, cols, width), keys.dtype),
            pltpu.VMEM((rows, cols), values.dtype),
            pltpu.VMEM((rows, width), jnp.float32),
            pltpu.VMEM((rows, width), jnp.float32),
            pltpu.VMEM((rows, width), jnp.float32),
            pltpu.SemaphoreType.DMA((3,)),
            pltpu.SemaphoreType.DMA((2, n, 4)),
            pltpu.SemaphoreType.DMA((n, 4)),
        ],
        compiler_params=pltpu.CompilerParams(collective_id=0, has_side_effects=True),
    )(
        block_order,
        queries.reshape(rows, width),
        keys.reshape(cols, width),
        values.reshape(cols, width),
    )
    return out.reshape(tokens, heads, width)


def solution(mesh):
    placed = P(("grp", "seq"), "head", None)
    return jax.shard_map(
        on_device,
        mesh=mesh,
        in_specs=(placed, placed, placed, P("grp")),
        out_specs=placed,
        check_vma=False,
    )
```

time: 34.1 us -> 20.9 us (0.61)
  Pallas kernels: 0 us -> 19.1 us
  matrix products: 13.6 us -> 0 us
  starting transfers between devices: 10.1 us -> 0 us
  waiting for transfers between devices: 4.23 us -> 0 us
  other arithmetic: 2.32 us -> 0 us
  local copies, waits for them, and re-layouts: 3.22 us -> 1.67 us
  between operations: 0.38 us -> 0.01 us
    pallas_call x0 -> x1, Pallas kernels: none -> 19.1 us  [on_device(): pl.pallas_call(functools.partial(gather_attend, n, heads, groups, tile),...]
    dot_general x64 -> x0, matrix products: 13.6 us -> none  [the longest x32 6.99 us: attend(): jnp.einsum('ghcp,pgd->ghcd', weights.astype(jnp.bfloat16), value_rows, pr...]
    ppermute x6 -> x0, starting transfers between devices: 10.1 us -> none  [the longest x4 6.91 us: partner(): return lax.ppermute(value, axis, pairs)]
    ppermute x6 -> x0, waiting for transfers between devices: 4.23 us -> none  [the longest x4 4.22 us: partner(): return lax.ppermute(value, axis, pairs)]
    reduce_sum x33 -> x0, other arithmetic: 1.65 us -> none  [the longest x32 1.57 us: attend(): new_sum = running_sum * factor + jnp.sum(weights, axis=-1)]
    dynamic_slice x3 -> x0, local copies, waits for them, and re-layouts: 1.45 us -> none  [the longest x1 1.17 us: on_device(): lax.dynamic_slice_in_dim(queries, parity * half_heads, half_heads, 1)]
    unnamed x12 -> x1, local copies, waits for them, and re-layouts: 0.75 us -> 1.67 us
    select_n x1 -> x0, local copies, waits for them, and re-layouts: 0.88 us -> none  [on_device(): jnp.where(lower, jnp.concatenate([mine, returned], 1), jnp.concatenate([r...]
  transfers between devices with their start and end apart: 6 -> 0, of which waited for: 2 -> 0; matrix products, arithmetic and copies ran while one was open for 38% -> 0% of each run, Pallas kernels for 0% -> 0%
where the time goes in v1:
time: 20.9 us; the launch traced here: 20.8 us
  Pallas kernels  19.1 us (91%)
  local copies, waits for them, and re-layouts  1.67 us (8%)
    pallas_call x1, Pallas kernels, on_device(): pl.pallas_call(functools.partial(gather_attend, n, heads, groups, tile),...  19.1 us
    unnamed x1, local copies, waits for them, and re-layouts  1.67 us

profile of v1, /device:TPU:0, one launch (start us, length us, event | category | flops | bytes accessed | tf_op | source)
XLA Modules:
  0.0 20.8 jit_solution(15095344257993425646)
XLA Ops:
  0.0 19.1 %shard_map.46 = bf16[1024,128]{1,0:T(8,128)(2,1)} custom-call(s32[8]{0:T(128)} %table_ref.1, bf16[1024,128]{1,0:T(8,128)(2,1)} %bitcast.5, bf16[256,128]{1,0:T(8,128)(2,1)} %bitcast.6, bf16[256,128]{1,0:T(8,128)(2,1)} %bitcast.7), custom_call_target="tpu_custom_call" | custom-call | tf_op jit(solution)/shard_map/pallas_call | solution.py:230
  19.1 1.7 %copy.6 = bf16[128,8,128]{2,1,0:T(8,128)(2,1)} copy(bf16[128,8,128]{2,1,0:T(8,128)(2,1)} %bitcast.4) | data formatting | bytes 524288

commit v2 on v1

v2 whole, which is shorter than its diff:
```python
import functools
import math

import jax
import jax.numpy as jnp
from jax import lax
from jax.experimental import pallas as pl
from jax.experimental.pallas import tpu as pltpu
from jax.sharding import PartitionSpec as P

MESH = pl.DeviceIdType.MESH
NEG = -1e30


def gather_attend(
    n,
    heads,
    groups,
    tile,
    table_hbm,
    q_hbm,
    k_hbm,
    v_hbm,
    out_ref,
    table_ref,
    q_ref,
    kv_ref,
    p_ref,
    m_ref,
    l_ref,
    acc_ref,
    load_sem,
    send_sem,
    recv_sem,
):
    me = lax.axis_index("seq")
    rows, width = q_ref.shape
    tokens = rows // heads
    half = tokens // 2
    per_group = heads // groups
    cols = tokens * groups
    piece = cols // 2
    factor_scale = width ** (-0.5) * math.log2(math.e)
    right, left = me + 1, me - 1
    has_right, has_left = me < n - 1, me > 0
    barrier = pltpu.get_barrier_semaphore()

    @pl.when(has_right)
    def _():
        pl.semaphore_signal(barrier, inc=1, device_id={"seq": right}, device_id_type=MESH)

    @pl.when(has_left)
    def _():
        pl.semaphore_signal(barrier, inc=1, device_id={"seq": left}, device_id_type=MESH)

    loads = [
        pltpu.make_async_copy(k_hbm, kv_ref.at[me, 0], load_sem.at[0]),
        pltpu.make_async_copy(v_hbm, kv_ref.at[me, 1], load_sem.at[1]),
        pltpu.make_async_copy(table_hbm, table_ref, load_sem.at[2]),
        pltpu.make_async_copy(q_hbm, q_ref, load_sem.at[3]),
    ]
    for load in loads:
        load.start()

    pl.semaphore_wait(barrier, has_right.astype(jnp.int32) + has_left.astype(jnp.int32))

    def remote(shard, which, way):
        part = kv_ref.at[shard, which // 2, pl.ds((which % 2) * piece, piece)]
        return pltpu.make_async_remote_copy(
            src_ref=part,
            dst_ref=part,
            send_sem=send_sem.at[way, shard, which],
            recv_sem=recv_sem.at[shard, which],
            device_id={"seq": left if way else right},
            device_id_type=MESH,
        )

    for which in range(4):
        if which % 2 == 0:
            loads[which // 2].wait()

        @pl.when(has_right)
        def _():
            remote(me, which, 0).start()

        @pl.when(has_left)
        def _():
            remote(me, which, 1).start()

    m_ref[...] = jnp.full(m_ref.shape, NEG, jnp.float32)
    l_ref[...] = jnp.zeros(l_ref.shape, jnp.float32)
    acc_ref[...] = jnp.zeros(acc_ref.shape, jnp.float32)
    loads[2].wait()
    loads[3].wait()

    lane = lax.broadcasted_iota(jnp.int32, (heads, cols), 1)
    head = lax.broadcasted_iota(jnp.int32, (heads, cols), 0)
    matched = lane % groups == head // per_group
    key_token = lane // groups

    def take(distance, which):
        from_left, from_right = me - distance, me + distance

        @pl.when(from_left >= 0)
        def _():
            remote(from_left, which, 0).wait_recv()

            @pl.when(has_right)
            def _():
                remote(from_left, which, 0).start()

        @pl.when(from_right < n)
        def _():
            remote(from_right, which, 1).wait_recv()

            @pl.when(has_left)
            def _():
                remote(from_right, which, 1).start()

    def scores(shard, section, start):
        span = pl.ds(pl.multiple_of((section * half + start) * heads, tile * heads), tile * heads)
        first, second = table_ref[2 * shard], table_ref[2 * shard + 1]
        key_pos = jnp.where(
            key_token < half, first * half + key_token, (second - 1) * half + key_token
        )
        key_code = jnp.where(matched, key_pos, 2**30)
        offset = table_ref[2 * me + section] * half + start
        raw = lax.dot_general(
            q_ref[span, :],
            kv_ref[shard, 0],
            (((1,), (1,)), ((), ())),
            preferred_element_type=jnp.float32,
        )
        shaped = raw.reshape(tile, heads, cols)
        query_pos = lax.broadcasted_iota(jnp.int32, shaped.shape, 0) + offset
        shaped = jnp.where(key_code[None] <= query_pos, shaped, NEG)
        raw = shaped.reshape(tile * heads, cols)
        old_max = m_ref[span, :]
        new_max = jnp.maximum(old_max, jnp.max(raw, axis=-1, keepdims=True))
        fade = jnp.exp2((old_max - new_max) * factor_scale)
        total = l_ref[span, :] * fade
        pieces = []
        for low in range(0, cols, width):
            weights = jnp.exp2((raw[:, low : low + width] - new_max) * factor_scale)
            total += weights
            pieces.append(weights.astype(p_ref.dtype))
        m_ref[span, :] = new_max
        l_ref[span, :] = total
        return span, jnp.concatenate(pieces, axis=1), fade

    def both(shard, section):
        for start in range(0, half, tile):
            span, weights, fade = scores(shard, section, start)
            acc_ref[span, :] = acc_ref[span, :] * fade + jnp.dot(
                weights, kv_ref[shard, 1], preferred_element_type=jnp.float32
            )

    def own(section, carry):
        both(me, section)
        return carry

    lax.fori_loop(0, 2, own, 0)

    def catch_up(distance, section):
        def side(way, carry):
            shard = jnp.where(way == 0, me - distance, me + distance)

            @pl.when((distance > 0) & (shard >= 0) & (shard < n))
            def _():
                both(shard, section)

            return carry

        lax.fori_loop(0, 2, side, 0)

    def round_of(distance, carry):
        def section_of(section, carry):
            take(distance, section)
            catch_up(distance - 1, section)
            return carry

        lax.fori_loop(0, 2, section_of, 0)

        @pl.when((distance < n - 1) | (has_left & has_right))
        def _():
            for which in (2, 3):
                take(distance, which)

        return carry

    lax.fori_loop(1, n, round_of, 0)

    at_end = jnp.logical_not(has_left & has_right)
    if n > 1:

        @pl.when(at_end)
        def _():
            last = n - 1 - me
            for section in range(2):
                for start in range(0, half, tile):
                    span, weights, fade = scores(last, section, start)
                    p_ref[span, :] = weights
                    acc_ref[span, :] = acc_ref[span, :] * fade
            for which in (2, 3):
                take(n - 1, which)
            for start in range(0, tokens, tile):
                span = pl.ds(start * heads, tile * heads)
                acc_ref[span, :] += jnp.dot(
                    p_ref[span, :], kv_ref[last, 1], preferred_element_type=jnp.float32
                )

    for start in range(0, tokens, tile):
        span = pl.ds(start * heads, tile * heads)
        total = jnp.sum(l_ref[span, :], axis=-1, keepdims=True)
        out_ref[span, :] = (acc_ref[span, :] / total).astype(out_ref.dtype)

    def settle(distance, carry):
        for which in range(4):

            @pl.when((me - distance >= 0) & has_right)
            def _():
                remote(me - distance, which, 0).wait_send()

            @pl.when((me + distance < n) & has_left)
            def _():
                remote(me + distance, which, 1).wait_send()

        return carry

    lax.fori_loop(0, n, settle, 0)


def on_device(queries, keys, values, block_order):
    n = lax.axis_size("seq")
    tokens, heads, width = queries.shape
    groups = keys.shape[1]
    rows, cols = tokens * heads, tokens * groups
    tile = min(32, tokens // 2)
    anywhere = pl.BlockSpec(memory_space=pltpu.HBM)
    out = pl.pallas_call(
        functools.partial(gather_attend, n, heads, groups, tile),
        out_shape=pltpu.VMEM((rows, width), queries.dtype),
        in_specs=[anywhere] * 4,
        out_specs=pl.BlockSpec(memory_space=pltpu.VMEM),
        scratch_shapes=[
            pltpu.SMEM(block_order.shape, block_order.dtype),
            pltpu.VMEM((rows, width), queries.dtype),
            pltpu.VMEM((n, 2, cols, width), keys.dtype),
            pltpu.VMEM((rows, cols), values.dtype),
            pltpu.VMEM((rows, width), jnp.float32),
            pltpu.VMEM((rows, width), jnp.float32),
            pltpu.VMEM((rows, width), jnp.float32),
            pltpu.SemaphoreType.DMA((4,)),
            pltpu.SemaphoreType.DMA((2, n, 4)),
            pltpu.SemaphoreType.DMA((n, 4)),
        ],
        compiler_params=pltpu.CompilerParams(collective_id=0, has_side_effects=True),
    )(
        block_order,
        queries.reshape(rows, width),
        keys.reshape(cols, width),
        values.reshape(cols, width),
    )
    return out.reshape(tokens, heads, width)


def solution(mesh):
    placed = P(("grp", "seq"), "head", None)
    return jax.shard_map(
        on_device,
        mesh=mesh,
        in_specs=(placed, placed, placed, P("grp")),
        out_specs=placed,
        check_vma=False,
    )
```

time: 20.9 us -> 18.3 us (0.88)
  Pallas kernels: 19.1 us -> 17.5 us
  local copies, waits for them, and re-layouts: 1.67 us -> 0.71 us
    pallas_call x1, Pallas kernels: 19.1 us -> 17.5 us  [on_device(): pl.pallas_call(functools.partial(gather_attend, n, heads, groups, tile),...]
    unnamed x1, local copies, waits for them, and re-layouts: 1.67 us -> 0.71 us
where the time goes in v2:
time: 18.3 us; the launch traced here: 18.2 us
  Pallas kernels  17.5 us (96%)
  local copies, waits for them, and re-layouts  0.71 us (4%)
    pallas_call x1, Pallas kernels, on_device(): pl.pallas_call(functools.partial(gather_attend, n, heads, groups, tile),...  17.5 us
    unnamed x1, local copies, waits for them, and re-layouts  0.71 us

profile of v2, /device:TPU:0, one launch (start us, length us, event | category | flops | bytes accessed | tf_op | source)
XLA Modules:
  0.0 18.2 jit_solution(12721545058473313835)
XLA Ops:
  0.0 17.5 %shard_map.46 = bf16[1024,128]{1,0:T(8,128)(2,1)S(1)} custom-call(s32[8]{0:T(128)} %table_hbm.1, bf16[1024,128]{1,0:T(8,128)(2,1)} %bitcast.5, bf16[256,128]{1,0:T(8,128)(2,1)} %bitcast.6, bf16[256,128]{1,0:T(8,128)(2,1)} %bitcast.7), custom_call_target="tpu_custom_call" | custom-call | tf_op jit(solution)/shard_map/pallas_call | solution.py:240
  17.5 0.7 %copy.6 = bf16[128,8,128]{2,1,0:T(8,128)(2,1)} copy(bf16[128,8,128]{2,1,0:T(8,128)(2,1)S(1)} %bitcast.4) | data formatting | bytes 524288

commit v3 on v2

--- a/solution.py
+++ b/solution.py
@@ -43,6 +43,7 @@
     factor_scale = width ** (-0.5) * math.log2(math.e)
     right, left = me + 1, me - 1
     has_right, has_left = me < n - 1, me > 0
+    early = True
     barrier = pltpu.get_barrier_semaphore()
 
     @pl.when(has_right)
@@ -148,71 +149,48 @@
         l_ref[span, :] = total
         return span, jnp.concatenate(pieces, axis=1), fade
 
-    def both(shard, section):
-        for start in range(0, half, tile):
-            span, weights, fade = scores(shard, section, start)
-            acc_ref[span, :] = acc_ref[span, :] * fade + jnp.dot(
-                weights, kv_ref[shard, 1], preferred_element_type=jnp.float32
-            )
-
-    def own(section, carry):
-        both(me, section)
+    def both(shard, section, start):
+        span, weights, fade = scores(shard, section, start)
+        acc_ref[span, :] = acc_ref[span, :] * fade + jnp.dot(
+            weights, kv_ref[shard, 1], preferred_element_type=jnp.float32
+        )
+
+    def whole(shard):
+        def section_of(section, carry):
+            for start in range(0, half, tile):
+                both(shard, section, start)
+            return carry
+
+        lax.fori_loop(0, 2, section_of, 0)
+
+    whole(me)
+
+    def at(index, way):
+        return jnp.where(way == 0, me - index, me + index)
+
+    def relay_round(distance, carry):
+        def side(way):
+            shard = at(distance - 1, way)
+
+            @pl.when((distance > 1) & (shard >= 0) & (shard < n))
+            def _():
+                whole(shard)
+
+        if early:
+            side(0)
+        for which in range(4):
+            take(distance, which)
+        if not early:
+            side(0)
+        side(1)
         return carry
 
-    lax.fori_loop(0, 2, own, 0)
-
-    def catch_up(distance, section):
-        def side(way, carry):
-            shard = jnp.where(way == 0, me - distance, me + distance)
-
-            @pl.when((distance > 0) & (shard >= 0) & (shard < n))
-            def _():
-                both(shard, section)
-
-            return carry
-
-        lax.fori_loop(0, 2, side, 0)
-
-    def round_of(distance, carry):
-        def section_of(section, carry):
-            take(distance, section)
-            catch_up(distance - 1, section)
-            return carry
-
-        lax.fori_loop(0, 2, section_of, 0)
-
-        @pl.when((distance < n - 1) | (has_left & has_right))
-        def _():
-            for which in (2, 3):
-                take(distance, which)
-
+    def end_round(distance, carry):
+        shard = jnp.where(has_left, me - distance, me + distance)
+        for which in range(4):
+            take(distance, which)
+        whole(shard)
         return carry
-
-    lax.fori_loop(1, n, round_of, 0)
-
-    at_end = jnp.logical_not(has_left & has_right)
-    if n > 1:
-
-        @pl.when(at_end)
-        def _():
-            last = n - 1 - me
-            for section in range(2):
-                for start in range(0, half, tile):
-                    span, weights, fade = scores(last, section, start)
-                    p_ref[span, :] = weights
-                    acc_ref[span, :] = acc_ref[span, :] * fade
-            for which in (2, 3):
-                take(n - 1, which)
-            for start in range(0, tokens, tile):
-                span = pl.ds(start * heads, tile * heads)
-                acc_ref[span, :] += jnp.dot(
-                    p_ref[span, :], kv_ref[last, 1], preferred_element_type=jnp.float32
-                )
-
-    for start in range(0, tokens, tile):
-        span = pl.ds(start * heads, tile * heads)
-        total = jnp.sum(l_ref[span, :], axis=-1, keepdims=True)
-        out_ref[span, :] = (acc_ref[span, :] / total).astype(out_ref.dtype)
 
     def settle(distance, carry):
         for which in range(4):
@@ -227,7 +205,45 @@
 
         return carry
 
-    lax.fori_loop(0, n, settle, 0)
+    def close():
+        for start in range(0, tokens, tile):
+            span = pl.ds(start * heads, tile * heads)
+            scale = 1.0 / jnp.sum(l_ref[span, :], axis=-1, keepdims=True)
+            out_ref[span, :] = (acc_ref[span, :] * scale).astype(out_ref.dtype)
+
+    if n == 1:
+        close()
+        return
+
+    interior = has_left & has_right
+
+    @pl.when(interior)
+    def _():
+        lax.fori_loop(1, n - 1, relay_round, 0)
+        lax.fori_loop(0, n - 2, settle, 0)
+        relay_round(n - 1, 0)
+        close()
+        settle(n - 2, 0)
+
+    @pl.when(jnp.logical_not(interior))
+    def _():
+        lax.fori_loop(1, n - 1, end_round, 0)
+        settle(0, 0)
+        last = n - 1 - me
+        for which in (0, 1):
+            take(n - 1, which)
+        for start in range(0, tokens, tile):
+            span, weights, fade = scores(last, start // half, start % half)
+            scale = 1.0 / jnp.sum(l_ref[span, :], axis=-1, keepdims=True)
+            p_ref[span, :] = weights
+            acc_ref[span, :] = acc_ref[span, :] * (fade * scale)
+            l_ref[span, :] = jnp.broadcast_to(scale, (tile * heads, width))
+        for which in (2, 3):
+            take(n - 1, which)
+        for start in range(0, tokens, tile):
+            span = pl.ds(start * heads, tile * heads)
+            product = jnp.dot(p_ref[span, :], kv_ref[last, 1], preferred_element_type=jnp.float32)
+            out_ref[span, :] = (acc_ref[span, :] + product * l_ref[span, :]).astype(out_ref.dtype)
 
 
 def on_device(queries, keys, values, block_order):
@@ -235,7 +251,7 @@
     tokens, heads, width = queries.shape
     groups = keys.shape[1]
     rows, cols = tokens * heads, tokens * groups
-    tile = min(32, tokens // 2)
+    tile = min(64, tokens // 2)
     anywhere = pl.BlockSpec(memory_space=pltpu.HBM)
     out = pl.pallas_call(
         functools.partial(gather_attend, n, heads, groups, tile),

time: 18.3 us -> 15.9 us (0.87)
  Pallas kernels: 17.5 us -> 15.1 us
    pallas_call x1, Pallas kernels: 17.5 us -> 15.1 us  [on_device(): pl.pallas_call(functools.partial(gather_attend, n, heads, groups, tile),...]
where the time goes in v3:
time: 15.9 us; the launch traced here: 15.8 us
  Pallas kernels  15.1 us (95%)
  local copies, waits for them, and re-layouts  0.71 us (4%)
    pallas_call x1, Pallas kernels, on_device(): pl.pallas_call(functools.partial(gather_attend, n, heads, groups, tile),...  15.1 us
    unnamed x1, local copies, waits for them, and re-layouts  0.71 us

profile of v3, /device:TPU:0, one launch (start us, length us, event | category | flops | bytes accessed | tf_op | source)
XLA Modules:
  0.0 15.8 jit_solution(10205326000518844056)
XLA Ops:
  0.0 15.1 %shard_map.46 = bf16[1024,128]{1,0:T(8,128)(2,1)S(1)} custom-call(s32[8]{0:T(128)} %table_hbm.1, bf16[1024,128]{1,0:T(8,128)(2,1)} %bitcast.5, bf16[256,128]{1,0:T(8,128)(2,1)} %bitcast.6, bf16[256,128]{1,0:T(8,128)(2,1)} %bitcast.7), custom_call_target="tpu_custom_call" | custom-call | tf_op jit(solution)/shard_map/pallas_call | solution.py:256
  15.1 0.7 %copy.6 = bf16[128,8,128]{2,1,0:T(8,128)(2,1)} copy(bf16[128,8,128]{2,1,0:T(8,128)(2,1)S(1)} %bitcast.4) | data formatting | bytes 524288
